TPU v7x, 32 devices: a whole 2x2x4 slice. The times are simulated.
32 devices in a mesh: expert: 8 (over z, core), row: 4 (over y, x).
Axes of the slice: x: 2, y: 2, z: 4, core: 2. Of those that a mesh axis runs over, the one named last changes fastest.
Arguments:
- grads: bfloat16 [8, 7168, 2048], P('expert', 'row')
- basis: bfloat16 [8, 7168, 256], P('expert', 'row'), may hold values from -0.0625 to 0.0625
- loads: int32 [8], P('expert'), may hold values from 1 to 1, as said below
- flags: int32 [8], P('expert'), may hold values 0 or 1
Outputs:
- new_basis: float32 [8, 7168, 256], P('expert', 'row')
- rotated: float32 [8, 256, 2048], P('expert', None, 'row')
Inputs may be any that keep to these rules, and one draw needn't show every extreme that they name: Slots 0 to loads[d] - 1 of expert-axis index d are live and hold experts; the others are empty. Some index has all 1 slots live.
All inputs are finite; a program needn't handle non-finite values. No bound on the sum of `flags` on one device may be relied on, other than what follows from the above.
Results may differ from a plain program's by a relative error of at most 0.006.
Values sent between devices are 32-bit elements; how exact they have to be, the bound alone decides.
A program may use at most 64 MiB of HBM per device.

v0:
```python
import jax
import jax.numpy as jnp
from jax import lax
from jax.sharding import PartitionSpec as P

D = 7168
S = 2048


def on_device(grads, basis, loads, flags):
    slot_count = grads.shape[0]
    live_count = loads[0]
    live_mask = jnp.arange(slot_count, dtype=jnp.int32) < live_count
    refresh = jnp.logical_and(live_mask, flags == 1)
    live_cube = live_mask[:, None, None]
    refresh_cube = refresh[:, None, None]
    squares = jnp.sum(jnp.where(live_cube, jnp.square(grads.astype(jnp.float32)), 0.0))
    leader = (lax.axis_index("row") == 0).astype(jnp.float32)
    total_sq, total_live = lax.psum(
        (squares, leader * live_count.astype(jnp.float32)), ("expert", "row")
    )
    norm_scale = lax.rsqrt(total_sq / (total_live * D * S) + 1e-06)
    local_inner = jnp.einsum("cds,cdk->csk", grads, basis, preferred_element_type=jnp.float32)
    inner_sum = jnp.stack([lax.psum(local_inner[0], "row")])
    inner_gram = jnp.einsum("csk,csj->ckj", inner_sum, inner_sum, precision=lax.Precision.HIGHEST)
    inner_half = inner_sum.astype(jnp.bfloat16)
    power_rows = jnp.einsum(
        "cds,csk->cdk", grads, inner_half, preferred_element_type=jnp.float32
    ).astype(jnp.bfloat16)
    projector = jnp.where(refresh_cube, power_rows, basis)
    local_cross = jnp.einsum("cdk,cds->cks", projector, grads, preferred_element_type=jnp.float32)
    identity = jnp.eye(basis.shape[2], dtype=jnp.float32)
    lower_first = jnp.linalg.cholesky(jnp.where(refresh_cube, inner_gram, identity))
    first_rows = lax.linalg.triangular_solve(
        lower_first, power_rows.astype(jnp.float32), left_side=False, lower=True, transpose_a=True
    )
    local_second = jnp.einsum(
        "cdk,cdj->ckj", first_rows, first_rows, precision=lax.Precision.HIGHEST
    )
    gram_again = lax.psum(local_second, "row")
    cross_cols = lax.psum_scatter(local_cross, "row", scatter_dimension=2, tiled=True)
    lower_second = jnp.linalg.cholesky(jnp.where(refresh_cube, gram_again, identity))
    fresh_basis = lax.linalg.triangular_solve(
        lower_second, first_rows, left_side=False, lower=True, transpose_a=True
    )
    half_solved = lax.linalg.triangular_solve(lower_first, cross_cols, left_side=True, lower=True)
    fresh_rot = lax.linalg.triangular_solve(lower_second, half_solved, left_side=True, lower=True)
    new_basis = jnp.where(
        refresh_cube, fresh_basis, jnp.where(live_cube, basis.astype(jnp.float32), 0.0)
    )
    rotated = jnp.where(refresh_cube, fresh_rot, jnp.where(live_cube, cross_cols, 0.0)) * norm_scale
    return (new_basis, rotated)


def solution(mesh):
    placed = (P("expert", "row", None), P("expert", "row", None), P("expert"), P("expert"))
    return jax.shard_map(
        on_device,
        mesh=mesh,
        in_specs=placed,
        out_specs=(P("expert", "row", None), P("expert", None, "row")),
        check_vma=False,
    )
```

profile of v0, /device:TPU:0, one launch (start us, length us, event | category | flops | bytes accessed | tf_op | source)
XLA Modules:
  0.0 307.3 jit_solution(6141670956639925859)
XLA Ops:
  7.2 6.8 %fusion.4 = f32[2048,256]{1,0:T(8,128)} fusion(bf16[1,1792,2048]{2,1,0:T(8,128)(2,1)} %param.9, bf16[1,1792,256]{2,1,0:T(8,128)(2,1)} %param.10), kind=kOutput, calls=%fused_computation.9 | convolution fusion | flops 1879048192 | bytes 10354688 | tf_op jit(solution)/shard_map/cds,cdk->csk/dot_general | solution.py:23
  14.1 1.1 copy-done.2
  15.2 1.1 copy.12
  17.7 68.7 %all-reduce.5.cloned.1.call-done = f32[2048,256]{1,0:T(8,128)} async-done(((f32[2048,256]{1,0:T(8,128)}), f32[2048,256]{1,0:T(8,128)}) %all-reduce.5.cloned.1.call-update) | async-done | bytes 2097168 | tf_op jit(solution)/shard_map/psum | solution.py:24
  86.4 5.7 %convolution_select_fusion = f32[256,256]{0,1:T(8,128)S(1)} fusion(f32[2048,256]{1,0:T(8,128)} %all-reduce.5.cloned.1.call-done, pred[]{:T(512)} %bitcast), kind=kOutput, calls=%fused_computation.32 | convolution fusion | flops 1610809344 | bytes 2359297 | tf_op jit(solution)/shard_map/csk,csj->ckj/dot_general | solution.py:25
  92.3 0.7 copy-done.3
  93.0 11.7 %custom-call.21 = f32[1,128,128]{2,1,0:T(8,128)S(1)} custom-call(f32[1,128,128]{2,1,0:T(8,128)S(1)} %cholesky.191), custom_call_target="Cholesky" | custom-call | tf_op jit(solution)/shard_map/jit(cholesky)/cholesky | solution.py:33
  104.7 9.8 %custom-call.22 = f32[1,1,128,128]{2,3,1,0:T(8,128)S(1)} custom-call(f32[1,1,128,128]{3,2,1,0:T(8,128)S(1)} %get-tuple-element.68), custom_call_target="InvertDiagBlocksLowerTriangular" | custom-call | tf_op jit(solution)/shard_map/jit(cholesky)/cholesky | solution.py:33
  114.6 1.0 bitcast_dynamic-update-slice_fusion.3
  115.6 1.1 fusion.27
  116.7 11.9 %custom-call.23 = f32[1,128,128]{2,1,0:T(8,128)S(1)} custom-call(f32[1,128,128]{2,1,0:T(8,128)S(1)} %fusion.27), custom_call_target="Cholesky" | custom-call | tf_op jit(solution)/shard_map/jit(cholesky)/cholesky | solution.py:33
  128.6 0.7 compare_reduce_fusion.2
  130.7 3.9 %while.8 = (s32[]{:T(128)}, f32[1,256,256]{2,1,0:T(8,128)S(1)}, s32[2,2]{1,0:T(2,128)S(1)}, f32[2,1,128,128]{3,2,1,0:T(8,128)S(1)}, s32[]{:T(128)}) while((s32[]{:T(128)}, f32[1,256,256]{2,1,0:T(8,128)S(1)}, s32[2,2]{1,0:T(2,128)S(1)}, f32[2,1,128,128]{3,2,1,0:T(8,128)S(1)}, s32[]{:T(128)}) %tuple.57), condition=%wide.while_cond, body=%wide.while_body.sunk | while | flops 2 | bytes 131181 | solution.py:34
  130.7 0.6 fusion.71
  131.3 1.4 bitcast_dynamic-update-slice_fusion.6
  132.7 0.6 fusion.71
  133.3 1.4 bitcast_dynamic-update-slice_fusion.6
  134.6 19.7 %custom-call.24 = f32[1,2,128,128]{2,3,1,0:T(8,128)S(1)} custom-call(f32[1,2,128,128]{3,2,1,0:T(8,128)S(1)} %bitcast.221), custom_call_target="InvertDiagBlocksLowerTriangular" | custom-call | tf_op jit(solution)/shard_map/triangular_solve/custom-call.0 | solution.py:34
  154.3 6.2 %fusion.53 = (f32[1,1792,256]{1,2,0:T(8,128)S(1)}, bf16[1,1792,256]{1,2,0:T(8,128)(2,1)}) fusion(bf16[1,1792,2048]{2,1,0:T(8,128)(2,1)} %param.9, f32[2048,256]{1,0:T(8,128)S(1)} %copy-done), kind=kOutput, calls=%fused_computation.99 | convolution fusion | flops 1880489984 | bytes 12189696 | tf_op jit(solution)/shard_map/cds,csk->cdk/dot_general | solution.py:27
  160.5 1.0 fusion.30
  161.5 1.0 fusion.16
  162.5 1.0 convolution_bitcast_fusion.2
  163.4 2.4 fusion.22
  165.9 6.8 %fusion.6 = f32[1,256,2048]{2,1,0:T(8,128)} fusion(bf16[1,1792,2048]{2,1,0:T(8,128)(2,1)} %param.9, bf16[1,1792,256]{1,2,0:T(8,128)(2,1)} %get-tuple-element.70, bf16[1,1792,256]{1,2,0:T(8,128)(2,1)S(1)} %copy.12, pred[]{:T(512)} %bitcast), kind=kOutput, calls=%fused_computation.11 | convolution fusion | flops 1879506944 | bytes 11272193 | tf_op jit(solution)/shard_map/cdk,cds->cks/dot_general | solution.py:31
  172.7 7.5 %select_reduce_fusion = f32[]{:T(128)} fusion(bf16[1,1792,2048]{2,1,0:T(8,128)(2,1)} %param.9, pred[]{:T(512)} %bitcast.40), kind=kLoop, calls=%fused_computation.4 | loop fusion | flops 14680063 | bytes 7340037 | tf_op jit(solution)/shard_map/reduce_sum | solution.py:17
  180.2 39.4 %all-reduce.1 = (f32[]{:T(128)}, f32[]{:T(128)}) all-reduce(f32[]{:T(128)} %select_reduce_fusion, f32[]{:T(128)S(6)} %mul.13), channel_id=1, replica_groups=mesh['expert'=8,'row'=4] {'expert','row'}, use_global_device_ids=true, to_apply=%region_8.12 | all-reduce | flops 2 | bytes 16 | tf_op jit(solution)/shard_map/psum | solution.py:19
  221.0 1.0 convert_select_fusion
  222.1 1.0 fusion.40
  223.1 12.3 %custom-call.25 = f32[1,128,128]{2,1,0:T(8,128)} custom-call(f32[1,128,128]{2,1,0:T(8,128)S(1)} %cholesky.194), custom_call_target="Cholesky" | custom-call | tf_op jit(solution)/shard_map/jit(cholesky)/cholesky | solution.py:42
  235.5 0.9 cholesky.185
  236.3 1.5 select_reduce_fusion.2
  237.8 11.3 %custom-call.26 = f32[1,1,128,128]{2,3,1,0:T(8,128)} custom-call(f32[1,1,128,128]{3,2,1,0:T(8,128)} %get-tuple-element.64), custom_call_target="InvertDiagBlocksLowerTriangular" | custom-call | tf_op jit(solution)/shard_map/jit(cholesky)/cholesky | solution.py:42
  249.1 1.0 bitcast_dynamic-update-slice_fusion.2
  250.2 0.9 fusion.28
  251.1 12.5 %custom-call.27 = f32[1,128,128]{2,1,0:T(8,128)S(1)} custom-call(f32[1,128,128]{2,1,0:T(8,128)} %fusion.28), custom_call_target="Cholesky" | custom-call | tf_op jit(solution)/shard_map/jit(cholesky)/cholesky | solution.py:42
  263.7 0.6 compare_reduce_fusion
  264.3 0.6 compare_reduce_fusion.1
  266.3 4.0 %while.9 = (s32[]{:T(128)}, f32[1,256,256]{2,1,0:T(8,128)S(1)}, s32[2,2]{1,0:T(2,128)S(1)}, f32[2,1,128,128]{3,2,1,0:T(8,128)S(1)}, s32[]{:T(128)}) while((s32[]{:T(128)}, f32[1,256,256]{2,1,0:T(8,128)S(1)}, s32[2,2]{1,0:T(2,128)S(1)}, f32[2,1,128,128]{3,2,1,0:T(8,128)S(1)}, s32[]{:T(128)}) %tuple.69), condition=%wide.while_cond.clone, body=%wide.while_body.clone.sunk | while | flops 2 | bytes 131181 | solution.py:43
  266.9 1.4 bitcast_dynamic-update-slice_fusion.7
  268.9 1.4 bitcast_dynamic-update-slice_fusion.7
  270.3 19.9 %custom-call.28 = f32[1,2,128,128]{2,3,1,0:T(8,128)S(1)} custom-call(f32[1,2,128,128]{3,2,1,0:T(8,128)S(1)} %bitcast.220), custom_call_target="InvertDiagBlocksLowerTriangular" | custom-call | tf_op jit(solution)/shard_map/triangular_solve/custom-call.0 | solution.py:43
  290.2 0.9 fusion.31
  291.2 1.0 fusion.18
  292.1 1.0 convolution_bitcast_fusion
  293.3 1.7 copy.14
  295.0 1.4 fusion.38
  297.3 1.3 fusion.24
  299.5 0.9 fusion.37
  (44 shorter events, 3.8 us)
Async XLA Ops:
  7.2 79.2 %all-reduce.5.cloned.1.call-start = ((), (), s32[]{:S(2)}) async-start(), calls=%async_computation.1 | async-start | bytes 4194304 | tf_op jit(solution)/shard_map/psum | solution.py:24
  14.0 1.2 copy-start.2
  14.1 206.9 %all-reduce.7.cloned.1.call-start = ((), (), s32[]{:S(2)}) async-start(), calls=%async_computation.2 | async-start | bytes 524288 | tf_op jit(solution)/shard_map/psum | solution.py:40
  92.1 62.3 %copy-start = (f32[2048,256]{1,0:T(8,128)S(1)}, f32[2048,256]{1,0:T(8,128)}, u32[]{:S(2)}) copy-start(f32[2048,256]{1,0:T(8,128)} %all-reduce.5.cloned.1.call-done) | copy-start | bytes 6291460
  92.3 0.7 copy-start.3
  154.3 8.1 %copy-start.4 = (f32[1,2,128,128]{2,3,1,0:T(8,128)}, f32[1,2,128,128]{2,3,1,0:T(8,128)S(1)}, u32[]{:S(2)}) copy-start(f32[1,2,128,128]{2,3,1,0:T(8,128)S(1)} %custom-call.24) | copy-start | bytes 393220
  165.8 129.2 %reduce-scatter.2.cloned.1.call-start = ((), (), s32[]{:S(2)}) async-start(), calls=%async_computation.3 | async-start | bytes 2621440 | tf_op jit(solution)/shard_map/reduce_scatter | solution.py:41
  293.3 1.7 copy-start.5
  295.0 4.4 %copy-start.1 = (f32[1,256,512]{2,1,0:T(8,128)S(1)}, f32[1,256,512]{2,1,0:T(8,128)}, u32[]{:S(2)}) copy-start(f32[1,256,512]{2,1,0:T(8,128)} %reduce-scatter.2.cloned.1.call-done) | copy-start | bytes 1572868
Sparse Core Ops, SparseCore 0:
  14.2 72.1 all-reduce.4
  165.9 43.0 all-reduce.6
  211.9 35.2 reduce-scatter.1
where the time goes:
time: 311 us; the launch traced here: 307 us
  other arithmetic  123 us (40%)
  waiting for transfers between devices  68.8 us (22%)
  matrix products  42 us (14%)
  blocking collectives  39.4 us (13%)
  between operations  19.7 us (6%)
  local copies, waits for them, and re-layouts  13.7 us (4%)
    psum x1, waiting for transfers between devices, on_device(): inner_sum = jnp.stack([lax.psum(local_inner[0], 'row')])  68.7 us
    psum x1, blocking collectives, on_device(): lax.psum((squares, leader * live_count.astype(jnp.float32)), ('expert', '...  39.4 us
    another operation x7, other arithmetic, on_device(): jnp.linalg.cholesky(jnp.where(refresh_cube, gram_again, identity))  39 us
    another operation x6, other arithmetic, on_device(): jnp.linalg.cholesky(jnp.where(refresh_cube, inner_gram, identity))  34.1 us
    another operation x2, other arithmetic, on_device(): lax.linalg.triangular_solve(lower_second, first_rows, left_side=False, lo...  20 us
    another operation x3, other arithmetic, on_device(): lax.linalg.triangular_solve(lower_first, power_rows.astype(jnp.float32),...  19.7 us
    reduce_sum x1, other arithmetic, on_device(): jnp.sum(jnp.where(live_cube, jnp.square(grads.astype(jnp.float32)), 0.0))  7.48 us
    dot_general x1, matrix products, on_device(): jnp.einsum('cds,cdk->csk', grads, basis, preferred_element_type=jnp.float32)  6.82 us
  transfers between devices with their start and end apart: 3, of which 1 were waited for; matrix products, arithmetic and copies ran while one was open for 29% of the time, Pallas kernels for 0%

commit v1 on v0

--- a/solution.py
+++ b/solution.py
@@ -2,9 +2,16 @@
 import jax.numpy as jnp
 from jax import lax
 from jax.sharding import PartitionSpec as P
+from jax.lax import psum
 
 D = 7168
 S = 2048
+
+
+def obtain_sides_over_axis(local_block, which_axis, lane_axis):
+    for q in (which_axis, lane_axis):
+        local_block = psum(local_block, q)
+    return local_block
 
 
 def on_device(grads, basis, loads, flags):
@@ -16,8 +23,8 @@
     refresh_cube = refresh[:, None, None]
     squares = jnp.sum(jnp.where(live_cube, jnp.square(grads.astype(jnp.float32)), 0.0))
     leader = (lax.axis_index("row") == 0).astype(jnp.float32)
-    total_sq, total_live = lax.psum(
-        (squares, leader * live_count.astype(jnp.float32)), ("expert", "row")
+    total_sq, total_live = obtain_sides_over_axis(
+        (squares, leader * live_count.astype(jnp.float32)), "row", "expert"
     )
     norm_scale = lax.rsqrt(total_sq / (total_live * D * S) + 1e-06)
     local_inner = jnp.einsum("cds,cdk->csk", grads, basis, preferred_element_type=jnp.float32)

time: 311 us -> 299 us (0.961)
  blocking collectives: 39.4 us -> 24.1 us
  waiting for transfers between devices: 68.8 us -> 72.4 us
    psum x1 -> x2, blocking collectives: 39.4 us -> 24.1 us  [obtain_sides_over_axis(): local_block = psum(local_block, q)]
    psum x1, waiting for transfers between devices: 0.02 us -> 3.21 us  [on_device(): gram_again = lax.psum(local_second, 'row')]
  transfers between devices with their start and end apart: 3 -> 3, of which waited for: 1 -> 2; matrix products, arithmetic and copies ran while one was open for 29% -> 30% of each run, Pallas kernels for 0% -> 0%
where the time goes in v1:
time: 299 us; the launch traced here: 295 us
  other arithmetic  124 us (41%)
  waiting for transfers between devices  72.4 us (24%)
  matrix products  42 us (14%)
  blocking collectives  24.1 us (8%)
  between operations  19.5 us (7%)
  local copies, waits for them, and re-layouts  13.4 us (4%)
    psum x1, waiting for transfers between devices, on_device(): inner_sum = jnp.stack([lax.psum(local_inner[0], 'row')])  69.1 us
    another operation x7, other arithmetic, on_device(): jnp.linalg.cholesky(jnp.where(refresh_cube, gram_again, identity))  39 us
    another operation x6, other arithmetic, on_device(): jnp.linalg.cholesky(jnp.where(refresh_cube, inner_gram, identity))  34.4 us
    psum x2, blocking collectives, obtain_sides_over_axis(): local_block = psum(local_block, q)  24.1 us
    another operation x2, other arithmetic, on_device(): lax.linalg.triangular_solve(lower_second, first_rows, left_side=False, lo...  19.9 us
    another operation x3, other arithmetic, on_device(): lax.linalg.triangular_solve(lower_first, power_rows.astype(jnp.float32),...  19.7 us
    reduce_sum x1, other arithmetic, on_device(): jnp.sum(jnp.where(live_cube, jnp.square(grads.astype(jnp.float32)), 0.0))  7.49 us
    dot_general x1, matrix products, on_device(): jnp.einsum('cds,cdk->csk', grads, basis, preferred_element_type=jnp.float32)  6.82 us
  transfers between devices with their start and end apart: 3, of which 2 were waited for; matrix products, arithmetic and copies ran while one was open for 30% of the time, Pallas kernels for 0%

profile of v1, /device:TPU:0, one launch (start us, length us, event | category | flops | bytes accessed | tf_op | source)
XLA Modules:
  0.0 295.3 jit_solution(6003827231925301648)
XLA Ops:
  7.2 6.8 %fusion.4 = f32[2048,256]{1,0:T(8,128)} fusion(bf16[1,1792,2048]{2,1,0:T(8,128)(2,1)} %param.9, bf16[1,1792,256]{2,1,0:T(8,128)(2,1)} %param.10), kind=kOutput, calls=%fused_computation.9 | convolution fusion | flops 1879048192 | bytes 10354688 | tf_op jit(solution)/shard_map/cds,cdk->csk/dot_general | solution.py:30
  14.1 1.1 copy-done.2
  15.2 0.8 copy.12
  17.3 69.1 %all-reduce.6.cloned.1.call-done = f32[2048,256]{1,0:T(8,128)} async-done(((f32[2048,256]{1,0:T(8,128)}), f32[2048,256]{1,0:T(8,128)}) %all-reduce.6.cloned.1.call-update) | async-done | bytes 2097168 | tf_op jit(solution)/shard_map/psum | solution.py:31
  86.4 5.7 %convolution_select_fusion = f32[256,256]{0,1:T(8,128)S(1)} fusion(f32[2048,256]{1,0:T(8,128)} %all-reduce.6.cloned.1.call-done, pred[]{:T(512)} %bitcast), kind=kOutput, calls=%fused_computation.32 | convolution fusion | flops 1610809344 | bytes 2359297 | tf_op jit(solution)/shard_map/csk,csj->ckj/dot_general | solution.py:32
  92.3 0.7 copy-done.3
  93.0 11.7 %custom-call.21 = f32[1,128,128]{2,1,0:T(8,128)S(1)} custom-call(f32[1,128,128]{2,1,0:T(8,128)S(1)} %cholesky.191), custom_call_target="Cholesky" | custom-call | tf_op jit(solution)/shard_map/jit(cholesky)/cholesky | solution.py:40
  104.8 9.8 %custom-call.22 = f32[1,1,128,128]{2,3,1,0:T(8,128)S(1)} custom-call(f32[1,1,128,128]{3,2,1,0:T(8,128)S(1)} %get-tuple-element.70), custom_call_target="InvertDiagBlocksLowerTriangular" | custom-call | tf_op jit(solution)/shard_map/jit(cholesky)/cholesky | solution.py:40
  114.6 1.0 bitcast_dynamic-update-slice_fusion.3
  115.7 1.1 fusion.27
  116.8 12.1 %custom-call.23 = f32[1,128,128]{2,1,0:T(8,128)S(1)} custom-call(f32[1,128,128]{2,1,0:T(8,128)S(1)} %fusion.27), custom_call_target="Cholesky" | custom-call | tf_op jit(solution)/shard_map/jit(cholesky)/cholesky | solution.py:40
  128.9 0.7 compare_reduce_fusion.2
  130.9 3.9 %while.8 = (s32[]{:T(128)}, f32[1,256,256]{2,1,0:T(8,128)S(1)}, s32[2,2]{1,0:T(2,128)S(1)}, f32[2,1,128,128]{3,2,1,0:T(8,128)S(1)}, s32[]{:T(128)}) while((s32[]{:T(128)}, f32[1,256,256]{2,1,0:T(8,128)S(1)}, s32[2,2]{1,0:T(2,128)S(1)}, f32[2,1,128,128]{3,2,1,0:T(8,128)S(1)}, s32[]{:T(128)}) %tuple.57), condition=%wide.while_cond, body=%wide.while_body.sunk | while | flops 2 | bytes 131181 | solution.py:41
  131.6 1.4 bitcast_dynamic-update-slice_fusion.6
  133.5 1.4 bitcast_dynamic-update-slice_fusion.6
  134.9 19.7 %custom-call.24 = f32[1,2,128,128]{2,3,1,0:T(8,128)S(1)} custom-call(f32[1,2,128,128]{3,2,1,0:T(8,128)S(1)} %bitcast.221), custom_call_target="InvertDiagBlocksLowerTriangular" | custom-call | tf_op jit(solution)/shard_map/triangular_solve/custom-call.0 | solution.py:41
  154.6 6.2 %fusion.53 = (f32[1,1792,256]{1,2,0:T(8,128)S(1)}, bf16[1,1792,256]{1,2,0:T(8,128)(2,1)}) fusion(bf16[1,1792,2048]{2,1,0:T(8,128)(2,1)} %param.9, f32[2048,256]{1,0:T(8,128)S(1)} %copy-done), kind=kOutput, calls=%fused_computation.99 | convolution fusion | flops 1880489984 | bytes 12189696 | tf_op jit(solution)/shard_map/cds,csk->cdk/dot_general | solution.py:34
  160.8 1.0 fusion.30
  161.7 1.0 fusion.16
  162.7 1.0 convolution_bitcast_fusion.2
  163.7 2.4 fusion.22
  166.3 6.8 %fusion.6 = f32[1,256,2048]{2,1,0:T(8,128)} fusion(bf16[1,1792,2048]{2,1,0:T(8,128)(2,1)} %param.9, bf16[1,1792,256]{1,2,0:T(8,128)(2,1)} %get-tuple-element.72, bf16[1,1792,256]{1,2,0:T(8,128)(2,1)S(1)} %copy.12, pred[]{:T(512)} %bitcast), kind=kOutput, calls=%fused_computation.11 | convolution fusion | flops 1879506944 | bytes 11272193 | tf_op jit(solution)/shard_map/cdk,cds->cks/dot_general | solution.py:38
  173.1 7.5 %select_reduce_fusion = f32[]{:T(128)} fusion(bf16[1,1792,2048]{2,1,0:T(8,128)(2,1)} %param.9, pred[]{:T(512)} %bitcast.40), kind=kLoop, calls=%fused_computation.4 | loop fusion | flops 14680063 | bytes 7340037 | tf_op jit(solution)/shard_map/reduce_sum | solution.py:24
  180.6 9.6 %all-reduce.2 = (f32[]{:T(128)}, f32[]{:T(128)}) all-reduce(f32[]{:T(128)} %select_reduce_fusion, f32[]{:T(128)S(6)} %mul.13), channel_id=1, replica_groups=mesh['expert'=8,'row'=4] {'row'}, use_global_device_ids=true, to_apply=%region_8.12 | all-reduce | flops 2 | bytes 16 | tf_op jit(solution)/shard_map/psum | solution.py:13
  190.2 14.5 %all-reduce.1 = (f32[]{:T(128)}, f32[]{:T(128)}) all-reduce(f32[]{:T(128)} %get-tuple-element.57, f32[]{:T(128)} %get-tuple-element.58), channel_id=1, replica_groups=mesh['expert'=8,'row'=4] {'expert'}, use_global_device_ids=true, to_apply=%region_9.13 | all-reduce | flops 2 | bytes 16 | tf_op jit(solution)/shard_map/psum | solution.py:13
  206.1 3.2 %all-reduce.8.cloned.1.call-done = f32[1,256,256]{1,2,0:T(8,128)} async-done(((f32[1,256,256]{1,2,0:T(8,128)}), f32[1,256,256]{1,2,0:T(8,128)}) %all-reduce.8.cloned.1.call-update) | async-done | bytes 262160 | tf_op jit(solution)/shard_map/psum | solution.py:47
  209.3 1.0 convert_select_fusion
  210.4 1.0 fusion.40
  211.4 12.3 %custom-call.25 = f32[1,128,128]{2,1,0:T(8,128)} custom-call(f32[1,128,128]{2,1,0:T(8,128)S(1)} %cholesky.194), custom_call_target="Cholesky" | custom-call | tf_op jit(solution)/shard_map/jit(cholesky)/cholesky | solution.py:49
  223.7 0.9 cholesky.185
  224.6 1.5 select_reduce_fusion.2
  226.1 11.3 %custom-call.26 = f32[1,1,128,128]{2,3,1,0:T(8,128)} custom-call(f32[1,1,128,128]{3,2,1,0:T(8,128)} %get-tuple-element.66), custom_call_target="InvertDiagBlocksLowerTriangular" | custom-call | tf_op jit(solution)/shard_map/jit(cholesky)/cholesky | solution.py:49
  237.4 1.0 bitcast_dynamic-update-slice_fusion.2
  238.4 0.9 fusion.28
  239.3 12.5 %custom-call.27 = f32[1,128,128]{2,1,0:T(8,128)S(1)} custom-call(f32[1,128,128]{2,1,0:T(8,128)} %fusion.28), custom_call_target="Cholesky" | custom-call | tf_op jit(solution)/shard_map/jit(cholesky)/cholesky | solution.py:49
  251.9 0.6 compare_reduce_fusion
  252.6 0.6 compare_reduce_fusion.1
  254.6 4.0 %while.9 = (s32[]{:T(128)}, f32[1,256,256]{2,1,0:T(8,128)S(1)}, s32[2,2]{1,0:T(2,128)S(1)}, f32[2,1,128,128]{3,2,1,0:T(8,128)S(1)}, s32[]{:T(128)}) while((s32[]{:T(128)}, f32[1,256,256]{2,1,0:T(8,128)S(1)}, s32[2,2]{1,0:T(2,128)S(1)}, f32[2,1,128,128]{3,2,1,0:T(8,128)S(1)}, s32[]{:T(128)}) %tuple.69), condition=%wide.while_cond.clone, body=%wide.while_body.clone.sunk | while | flops 2 | bytes 131181 | solution.py:50
  255.2 1.4 bitcast_dynamic-update-slice_fusion.7
  257.2 1.4 bitcast_dynamic-update-slice_fusion.7
  258.6 19.9 %custom-call.28 = f32[1,2,128,128]{2,3,1,0:T(8,128)S(1)} custom-call(f32[1,2,128,128]{3,2,1,0:T(8,128)S(1)} %bitcast.220), custom_call_target="InvertDiagBlocksLowerTriangular" | custom-call | tf_op jit(solution)/shard_map/triangular_solve/custom-call.0 | solution.py:50
  278.5 0.9 fusion.31
  279.4 1.0 fusion.18
  280.4 1.0 convolution_bitcast_fusion
  281.6 1.7 copy.14
  283.2 1.4 fusion.38
  285.5 1.3 fusion.24
  287.7 0.9 fusion.37
  (45 shorter events, 5.1 us)
Async XLA Ops:
  7.2 79.3 %all-reduce.6.cloned.1.call-start = ((), (), s32[]{:S(2)}) async-start(), calls=%async_computation.1 | async-start | bytes 4194304 | tf_op jit(solution)/shard_map/psum | solution.py:31
  14.0 1.2 copy-start.2
  14.1 195.2 %all-reduce.8.cloned.1.call-start = ((), (), s32[]{:S(2)}) async-start(), calls=%async_computation.2 | async-start | bytes 524288 | tf_op jit(solution)/shard_map/psum | solution.py:47
  92.1 62.5 %copy-start = (f32[2048,256]{1,0:T(8,128)S(1)}, f32[2048,256]{1,0:T(8,128)}, u32[]{:S(2)}) copy-start(f32[2048,256]{1,0:T(8,128)} %all-reduce.6.cloned.1.call-done) | copy-start | bytes 6291460
  92.3 0.7 copy-start.3
  154.6 8.1 %copy-start.4 = (f32[1,2,128,128]{2,3,1,0:T(8,128)}, f32[1,2,128,128]{2,3,1,0:T(8,128)S(1)}, u32[]{:S(2)}) copy-start(f32[1,2,128,128]{2,3,1,0:T(8,128)S(1)} %custom-call.24) | copy-start | bytes 393220
  166.1 117.2 %reduce-scatter.2.cloned.1.call-start = ((), (), s32[]{:S(2)}) async-start(), calls=%async_computation.3 | async-start | bytes 2621440 | tf_op jit(solution)/shard_map/reduce_scatter | solution.py:48
  281.5 1.7 copy-start.5
  283.2 4.4 %copy-start.1 = (f32[1,256,512]{2,1,0:T(8,128)S(1)}, f32[1,256,512]{2,1,0:T(8,128)}, u32[]{:S(2)}) copy-start(f32[1,256,512]{2,1,0:T(8,128)} %reduce-scatter.2.cloned.1.call-done) | copy-start | bytes 1572868
Sparse Core Ops, SparseCore 0:
  14.2 72.1 all-reduce.5
  166.2 43.0 all-reduce.7
  212.2 35.3 reduce-scatter.1
